TPU v7x, 512 devices: a whole 4x8x8 slice. The times are simulated.
512 devices in a mesh: dp: 256 (over z, x, y), mp: 2 (over core).
Axes of the slice: x: 4, y: 8, z: 8, core: 2. Of those that a mesh axis runs over, the one named last changes fastest.
Arguments:
- normed: bfloat16 [98304, 2048], P(('dp', 'mp')), may hold values from -24 to 24
- key_grad: bfloat16 [98304, 512], P('dp', 'mp'), may hold values from -0.01953125 to 0.01953125
- stale: bfloat16 [256, 2048, 512], P('dp', None, 'mp'), may hold values from -0.375 to 0.375
- worker_flag: int32 [256], P('dp'), may hold values 0 or 1
- block_mask: int32 [256, 4], P('dp'), may hold values 0 or 1
- aggregate: float32 [2048, 512], P('dp', 'mp'), may hold values from -6 to 6
- master: float32 [2048, 512], P('dp', 'mp'), may hold values from -0.125 to 0.125
- moment_one: float32 [2048, 512], P('dp', 'mp'), may hold values from -6 to 6
- moment_two: float32 [2048, 512], P('dp', 'mp'), may hold values from 0.5 to 4
Outputs:
- new_aggregate: float32 [2048, 512], P('dp', 'mp')
- new_master: float32 [2048, 512], P('dp', 'mp')
- new_moment_one: float32 [2048, 512], P('dp', 'mp')
- new_moment_two: float32 [2048, 512], P('dp', 'mp')
- weights: bfloat16 [2048, 512], P(None, 'mp')
- new_stale: bfloat16 [256, 2048, 512], P('dp', None, 'mp')
All inputs are finite; a program needn't handle non-finite values. No bound on the sum of `worker_flag` on one device may be relied on, other than what follows from the above.
Results may differ from a plain program's by a relative error of at most 0.0004.
Values may be sent and summed in bfloat16 or wider, within the bound.
No kernel may reach another device: no remote copies, remote signals or barrier semaphores. Data moves between devices by JAX's collectives and lax.ppermute only.
A program may use at most 64 MiB of HBM per device.

v0:
```python
import jax
import jax.numpy as jnp
from jax import lax
from jax.sharding import Mesh
from jax.sharding import PartitionSpec as P

H = 512
BLOCKS = 4
STEP = 10
DP = ("dp_0", "dp_1", "dp_2")
DP_MP = ("dp_0", "dp_1", "dp_2", "mp")


beta_one = 0.9
beta_two = 0.95
learn_rate = 0.001
decay_rate = 0.1
epsilon = 1e-08


def copy_for_each(x, axis):
    copies = jnp.broadcast_to(x, (lax.axis_size(axis), *x.shape))
    return lax.all_to_all(copies, axis, split_axis=0, concat_axis=0, tiled=True)


def joined_along(pieces, dim):
    pieces = jnp.moveaxis(pieces, 0, dim)
    dims = pieces.shape
    return pieces.reshape(*dims[:dim], dims[dim] * dims[dim + 1], *dims[dim + 2 :])


def collect(x, axis, dim):
    pieces = copy_for_each(x, axis)
    return joined_along(pieces, dim)


def in_blocks(x, dim, size):
    before, after = (x.shape[:dim], x.shape[dim + 1 :])
    return jnp.moveaxis(x.reshape(*before, size, -1, *after), dim, 0)


def sent_and_summed(x, axis, dim):
    pieces = in_blocks(x, dim, lax.axis_size(axis))
    arrived = lax.all_to_all(pieces, axis, split_axis=0, concat_axis=0, tiled=True)
    return arrived.sum(axis=0)


def summed_rows(x, axes, dim):
    far, near = axes
    own = sent_and_summed(in_blocks(x, dim, lax.axis_size(far)), near, dim + 1)
    return jnp.sum(lax.all_to_all(own, far, 0, 0, tiled=True), axis=0)


def gathered_by_axis(x, axes, dim):
    far, near = axes
    leading = copy_for_each(x, far)
    pieces = jnp.swapaxes(copy_for_each(leading, near), 0, 1)
    return joined_along(pieces.reshape(-1, *x.shape), dim)


def on_device(
    normed, key_grad, stale, worker_flag, block_mask, aggregate, master, moment_one, moment_two
):
    half_cols = key_grad.shape[1]
    first_col = lax.axis_index("mp") * half_cols
    columns = first_col + jnp.arange(half_cols, dtype=jnp.int32)
    column_block = columns // (H // BLOCKS)
    onehot = (column_block[:, None] == jnp.arange(BLOCKS, dtype=jnp.int32)[None, :]).astype(
        jnp.int32
    )
    trig = worker_flag[0] * jnp.sum(onehot * block_mask[0][None, :], axis=1)
    weight = trig.astype(jnp.float32)
    gathered = collect(normed, "mp", 0)
    grad = lax.dot_general(
        gathered, key_grad, (((0,), (0,)), ((), ())), preferred_element_type=jnp.float32
    )
    old = stale[0]
    term = weight[None, :] * (grad - old.astype(jnp.float32))
    reduced = summed_rows(term, ("dp_0", ("dp_1", "dp_2")), 0)
    new_aggregate = aggregate + reduced
    new_moment_one = beta_one * moment_one + (1.0 - beta_one) * new_aggregate
    new_moment_two = beta_two * moment_two + (1.0 - beta_two) * new_aggregate * new_aggregate
    first_hat = new_moment_one / (1.0 - beta_one**STEP)
    second_hat = new_moment_two / (1.0 - beta_two**STEP)
    update = first_hat / (jnp.sqrt(second_hat) + epsilon)
    new_master = master - learn_rate * (update + decay_rate * master)
    fresh = new_master.astype(jnp.bfloat16)
    weights = gathered_by_axis(fresh, ("dp_0", ("dp_1", "dp_2")), 0)
    kept = jnp.where(trig[None, :] > 0, grad.astype(jnp.bfloat16), old)
    return (new_aggregate, new_master, new_moment_one, new_moment_two, weights, kept[None])


def solution(mesh):
    torus = Mesh(mesh.devices.reshape(8, 4, 8, mesh.shape["mp"]), ("dp_0", "dp_1", "dp_2", "mp"))
    return jax.shard_map(
        on_device,
        mesh=torus,
        in_specs=(
            P(DP_MP, None),
            P(DP, "mp"),
            P(DP, None, "mp"),
            P(DP),
            P(DP, None),
            P(DP, "mp"),
            P(DP, "mp"),
            P(DP, "mp"),
            P(DP, "mp"),
        ),
        out_specs=(
            P(DP, "mp"),
            P(DP, "mp"),
            P(DP, "mp"),
            P(DP, "mp"),
            P(None, "mp"),
            P(DP, None, "mp"),
        ),
        check_vma=False,
    )
```

profile of v0, /device:TPU:8, one launch (start us, length us, event | category | flops | bytes accessed | tf_op | source)
XLA Modules:
  0.0 135.5 jit_solution(12315041189508624701)
XLA Ops:
  0.6 0.0 copy-start
  0.6 2.5 %broadcast_in_dim.24 = bf16[2,192,2048]{2,1,0:T(8,128)(2,1)} broadcast(bf16[192,2048]{1,0:T(8,128)(2,1)} %param.9), dimensions={1,2} | broadcast | bytes 2359296 | tf_op jit(solution)/shard_map/broadcast_in_dim | solution.py:22
  3.2 0.0 copy-start.7
  3.2 0.0 copy-start.1
  3.2 3.8 %all-to-all-start = ((bf16[2,192,2048]{2,1,0:T(8,128)(2,1)}), bf16[2,192,2048]{2,1,0:T(8,128)(2,1)S(1)}, u32[]{:S(2)}, u32[]{:S(2)}) async-start(bf16[2,192,2048]{2,1,0:T(8,128)(2,1)} %broadcast_in_dim.24), calls=%async_computation | async-start | bytes 3145728 | tf_op jit(solution)/shard_map/all_to_all | solution.py:23
  7.7 0.0 copy-done.7
  7.7 0.1 select_reduce_fusion
  7.8 1.7 %all-to-all-done = bf16[2,192,2048]{2,1,0:T(8,128)(2,1)S(1)} async-done(((bf16[2,192,2048]{2,1,0:T(8,128)(2,1)}), bf16[2,192,2048]{2,1,0:T(8,128)(2,1)S(1)}, u32[]{:S(2)}, u32[]{:S(2)}) %all-to-all-start) | async-done | bytes 1572896 | tf_op jit(solution)/shard_map/all_to_all | solution.py:23
  9.5 0.0 copy-done
  9.5 0.0 copy-done.1
  9.5 1.7 %subtract_multiply_fusion = (f32[2048,256]{1,0:T(8,128)S(1)}, bf16[2048,256]{1,0:T(8,128)(2,1)}) fusion(bf16[1,2048,256]{2,1,0:T(8,128)(2,1)S(1)} %copy-done.1, f32[256]{0:T(256)S(1)} %multiply_convert_fusion, bf16[384,2048]{1,0:T(8,128)(2,1)S(1)} %bitcast.23, bf16[384,256]{1,0:T(8,128)(2,1)S(1)} %copy-done), kind=kOutput, calls=%fused_computation.1 | convolution fusion | flops 404750336 | bytes 5964800 | tf_op jit(solution)/shard_map/dot_general | solution.py:74
  11.2 0.3 copy.21
  11.5 61.2 %all_to_all.25 = f32[32,8,8,256]{3,2,1,0:T(8,128)S(1)} all-to-all(f32[32,8,8,256]{3,2,1,0:T(8,128)S(1)} %bitcast.22), channel_id=1, replica_groups=mesh['dp_0'=8,'dp_1'=4,'dp_2'=8,'mp'=2] {'dp_1','dp_2'}, dimensions={0} | all-to-all | bytes 4194304 | tf_op jit(solution)/shard_map/all_to_all | solution.py:44
  72.7 0.0 copy-start.3
  72.7 0.0 copy-start.4
  72.7 0.0 copy-start.5
  72.7 0.0 copy-start.6
  72.7 0.1 reduce_sum.28
  72.8 0.0 copy-start.2
  72.8 18.6 %all_to_all.26 = f32[8,8,256]{2,1,0:T(8,128)S(1)} all-to-all(f32[8,8,256]{2,1,0:T(8,128)S(1)} %reduce_sum.28), channel_id=1, replica_groups=mesh['dp_0'=8,'dp_1'=4,'dp_2'=8,'mp'=2] {'dp_0'}, dimensions={0} | all-to-all | bytes 131072 | tf_op jit(solution)/shard_map/all_to_all | solution.py:51
  91.5 0.0 copy-done.3
  91.5 0.0 copy-done.4
  91.5 0.0 copy-done.5
  91.5 0.0 copy-done.6
  91.5 0.6 fusion.2
  92.1 10.4 %all_to_all.27 = bf16[8,8,256]{2,1,0:T(8,128)(2,1)S(1)} all-to-all(bf16[8,8,256]{2,1,0:T(8,128)(2,1)S(1)} %broadcast_in_dim.25), channel_id=1, replica_groups=mesh['dp_0'=8,'dp_1'=4,'dp_2'=8,'mp'=2] {'dp_0'}, dimensions={0} | all-to-all | bytes 65536 | tf_op jit(solution)/shard_map/all_to_all | solution.py:23
  102.5 1.1 broadcast_in_dim.26
  103.6 5.2 %all-to-all-start.4 = ((bf16[32,8,8,256]{3,2,1,0:T(8,128)(2,1)}), bf16[32,8,8,256]{3,2,1,0:T(8,128)(2,1)S(1)}, u32[]{:S(2)}, u32[]{:S(2)}) async-start(bf16[32,8,8,256]{3,2,1,0:T(8,128)(2,1)} %broadcast_in_dim.26), calls=%async_computation.4 | async-start | bytes 2097152 | tf_op jit(solution)/shard_map/all_to_all | solution.py:23
  108.9 0.0 copy-done.2
  108.9 1.1 fusion
  110.0 24.5 %all-to-all-done.4 = bf16[32,8,8,256]{3,2,1,0:T(8,128)(2,1)S(1)} async-done(((bf16[32,8,8,256]{3,2,1,0:T(8,128)(2,1)}), bf16[32,8,8,256]{3,2,1,0:T(8,128)(2,1)S(1)}, u32[]{:S(2)}, u32[]{:S(2)}) %all-to-all-start.4) | async-done | bytes 1048608 | tf_op jit(solution)/shard_map/all_to_all | solution.py:23
  134.4 1.0 copy.19
  (5 shorter events, 0.0 us)
Async XLA Ops:
  0.6 8.8 %copy-start = (bf16[384,256]{1,0:T(8,128)(2,1)S(1)}, bf16[384,256]{1,0:T(8,128)(2,1)}, u32[]{:S(2)}) copy-start(bf16[384,256]{1,0:T(8,128)(2,1)} %param.10) | copy-start | bytes 589828
  3.2 4.5 %copy-start.7 = (s32[1,4]{1,0:T(1,128)S(1)}, s32[1,4]{1,0:T(1,128)}, u32[]{:S(2)}) copy-start(s32[1,4]{1,0:T(1,128)} %param.13) | copy-start | bytes 52
  3.2 6.3 %copy-start.1 = (bf16[1,2048,256]{2,1,0:T(8,128)(2,1)S(1)}, bf16[1,2048,256]{2,1,0:T(8,128)(2,1)}, u32[]{:S(2)}) copy-start(bf16[1,2048,256]{2,1,0:T(8,128)(2,1)} %param.11) | copy-start | bytes 3145732
  3.2 6.3 %all-to-all-start = ((bf16[2,192,2048]{2,1,0:T(8,128)(2,1)}), bf16[2,192,2048]{2,1,0:T(8,128)(2,1)S(1)}, u32[]{:S(2)}, u32[]{:S(2)}) async-start(bf16[2,192,2048]{2,1,0:T(8,128)(2,1)} %broadcast_in_dim.24), calls=%async_computation | async-start | bytes 3145728 | tf_op jit(solution)/shard_map/all_to_all | solution.py:23
  72.7 18.8 %copy-start.3 = (f32[8,256]{1,0:T(8,128)S(1)}, f32[8,256]{1,0:T(8,128)}, u32[]{:S(2)}) copy-start(f32[8,256]{1,0:T(8,128)} %param.15) | copy-start | bytes 24580
  72.7 18.8 %copy-start.4 = (f32[8,256]{1,0:T(8,128)S(1)}, f32[8,256]{1,0:T(8,128)}, u32[]{:S(2)}) copy-start(f32[8,256]{1,0:T(8,128)} %param.16) | copy-start | bytes 24580
  72.7 18.8 %copy-start.5 = (f32[8,256]{1,0:T(8,128)S(1)}, f32[8,256]{1,0:T(8,128)}, u32[]{:S(2)}) copy-start(f32[8,256]{1,0:T(8,128)} %param.17) | copy-start | bytes 24580
  72.7 18.8 %copy-start.6 = (f32[8,256]{1,0:T(8,128)S(1)}, f32[8,256]{1,0:T(8,128)}, u32[]{:S(2)}) copy-start(f32[8,256]{1,0:T(8,128)} %param.14) | copy-start | bytes 24580
  72.8 36.1 %copy-start.2 = (bf16[2048,256]{1,0:T(8,128)(2,1)S(1)}, bf16[2048,256]{1,0:T(8,128)(2,1)}, u32[]{:S(2)}) copy-start(bf16[2048,256]{1,0:T(8,128)(2,1)} %get-tuple-element.12) | copy-start | bytes 3145732
  103.6 30.8 %all-to-all-start.4 = ((bf16[32,8,8,256]{3,2,1,0:T(8,128)(2,1)}), bf16[32,8,8,256]{3,2,1,0:T(8,128)(2,1)S(1)}, u32[]{:S(2)}, u32[]{:S(2)}) async-start(bf16[32,8,8,256]{3,2,1,0:T(8,128)(2,1)} %broadcast_in_dim.26), calls=%async_computation.4 | async-start | bytes 2097152 | tf_op jit(solution)/shard_map/all_to_all | solution.py:23
where the time goes:
time: 136 us; the launch traced here: 135 us
  blocking collectives  90.2 us (66%)
  waiting for transfers between devices  26.2 us (19%)
  starting transfers between devices  9.04 us (7%)
  local copies, waits for them, and re-layouts  4.96 us (4%)
  other arithmetic  1.95 us (1%)
  matrix products  1.72 us (1%)
  between operations  1.4 us (1%)
    all_to_all x1, blocking collectives, sent_and_summed(): lax.all_to_all(pieces, axis, split_axis=0, concat_axis=0, tiled=True)  61.2 us
    all_to_all x2, waiting for transfers between devices, copy_for_each(): return lax.all_to_all(copies, axis, split_axis=0, concat_axis=0, tiled=True)  26.2 us
    all_to_all x1, blocking collectives, summed_rows(): return jnp.sum(lax.all_to_all(own, far, 0, 0, tiled=True), axis=0)  18.6 us
    all_to_all x1, blocking collectives, copy_for_each(): return lax.all_to_all(copies, axis, split_axis=0, concat_axis=0, tiled=True)  10.4 us
    all_to_all x2, starting transfers between devices, copy_for_each(): return lax.all_to_all(copies, axis, split_axis=0, concat_axis=0, tiled=True)  9.04 us
    broadcast_in_dim x3, local copies, waits for them, and re-layouts, copy_for_each(): copies = jnp.broadcast_to(x, (lax.axis_size(axis), *x.shape))  3.62 us
  transfers between devices with their start and end apart: 2, of which 2 were waited for; matrix products, arithmetic and copies ran while one was open for 1% of the time, Pallas kernels for 0%

commit v1 on v0

v1 whole, which is shorter than its diff:
```python
import jax
import jax.numpy as jnp
from jax import lax
from jax.experimental.layout import Layout, with_layout_constraint
from jax.sharding import Mesh
from jax.sharding import PartitionSpec as P

H = 512
BLOCKS = 4
STEP = 10
DP = ("zh", "zl", "x", "yh", "yl")
NEAR = ('x', 'yl')
FAR = ('zh', 'zl', 'yh')
NEAR_BACK = ('x', 'yl')
FAR_BACK = ('zh', 'zl', 'yh')
SCALE_ONE = 256.0
SCALE_TWO = 32.0

beta_one = 0.9
beta_two = 0.95
learn_rate = 0.001
decay_rate = 0.1
epsilon = 1e-08


def product(rows, cols):
    return lax.dot_general(rows, cols, (((0,), (0,)), ((), ())), preferred_element_type=jnp.float32)


def on_device(
    normed, key_grad, stale, worker_flag, block_mask, aggregate, master, moment_one, moment_two
):
    rows, half_cols = normed.shape[0], key_grad.shape[1]
    core = lax.axis_index("mp")
    first_col = core * half_cols
    columns = first_col + jnp.arange(half_cols, dtype=jnp.int32)
    column_block = columns // (H // BLOCKS)
    onehot = (column_block[:, None] == jnp.arange(BLOCKS, dtype=jnp.int32)[None, :]).astype(
        jnp.int32
    )
    trig = worker_flag[0] * jnp.sum(onehot * block_mask[0][None, :], axis=1)
    weight = trig.astype(jnp.float32) * SCALE_ONE
    other = lax.ppermute(normed, "mp", [(0, 1), (1, 0)])
    own_part = product(normed, lax.dynamic_slice_in_dim(key_grad, core * rows, rows, 0))
    grad = own_part + product(
        other, lax.dynamic_slice_in_dim(key_grad, (1 - core) * rows, rows, 0)
    )
    grad = with_layout_constraint(grad, Layout((0, 1)))
    old = stale[0]
    term = (weight[None, :] * (grad - old.astype(jnp.float32))).astype(jnp.float16)
    d = term.shape[0]
    sizes = tuple(lax.axis_size(a) for a in DP)
    n_near, n_far = lax.axis_size(NEAR), lax.axis_size(FAR)
    own = d // (n_near * n_far)
    order = [DP.index(a) for a in NEAR + FAR]
    pieces = term.reshape(*sizes, own, half_cols).transpose(*order, len(DP), len(DP) + 1)
    pieces = pieces.reshape(n_near, n_far * own, half_cols)
    near = lax.all_to_all(pieces, NEAR, 0, 0, tiled=True)
    partial = jnp.sum(near.astype(jnp.float32), axis=0) * (SCALE_TWO / SCALE_ONE)
    partial = partial.astype(jnp.float16).reshape(n_far, own, half_cols)
    far = lax.all_to_all(partial, FAR, 0, 0, tiled=True)
    reduced = jnp.sum(far.astype(jnp.float32), axis=0) * (1.0 / SCALE_TWO)
    new_aggregate = aggregate + reduced
    new_moment_one = beta_one * moment_one + (1.0 - beta_one) * new_aggregate
    new_moment_two = beta_two * moment_two + (1.0 - beta_two) * new_aggregate * new_aggregate
    first_hat = new_moment_one / (1.0 - beta_one**STEP)
    second_hat = new_moment_two / (1.0 - beta_two**STEP)
    update = first_hat / (jnp.sqrt(second_hat) + epsilon)
    new_master = master - learn_rate * (update + decay_rate * master)
    fresh = new_master.astype(jnp.bfloat16)
    n_near, n_far = lax.axis_size(NEAR_BACK), lax.axis_size(FAR_BACK)
    copies = jnp.broadcast_to(fresh, (n_far, own, half_cols))
    block = lax.all_to_all(copies, FAR_BACK, 0, 0, tiled=True).reshape(n_far * own, half_cols)
    copies = jnp.broadcast_to(block, (n_near, *block.shape))
    weights = lax.all_to_all(copies, NEAR_BACK, 0, 0, tiled=True)
    back = NEAR_BACK + FAR_BACK
    weights = weights.reshape(*(lax.axis_size(a) for a in back), own, half_cols)
    weights = weights.transpose(*(back.index(a) for a in DP), len(DP), len(DP) + 1)
    weights = weights.reshape(d, half_cols)
    kept = jnp.where(trig[None, :] > 0, grad.astype(jnp.bfloat16), old)
    return (new_aggregate, new_master, new_moment_one, new_moment_two, weights, kept[None])


def solution(mesh):
    torus = Mesh(mesh.devices.reshape(4, 2, 4, 4, 2, mesh.shape["mp"]), (*DP, "mp"))
    return jax.shard_map(
        on_device,
        mesh=torus,
        in_specs=(
            P((*DP, "mp"), None),
            P(DP, "mp"),
            P(DP, None, "mp"),
            P(DP),
            P(DP, None),
            P(DP, "mp"),
            P(DP, "mp"),
            P(DP, "mp"),
            P(DP, "mp"),
        ),
        out_specs=(
            P(DP, "mp"),
            P(DP, "mp"),
            P(DP, "mp"),
            P(DP, "mp"),
            P(None, "mp"),
            P(DP, None, "mp"),
        ),
        check_vma=False,
    )
```

time: 136 us -> 91.8 us (0.67)
  blocking collectives: 90.2 us -> 63.8 us
  waiting for transfers between devices: 26.2 us -> 10.8 us
  local copies, waits for them, and re-layouts: 4.96 us -> 2.38 us
  starting transfers between devices: 9.04 us -> 6.66 us
  matrix products: 1.72 us -> 3.62 us
    all_to_all x3, blocking collectives: 90.2 us -> 63.8 us  [the longest x1 24.5 us: on_device(): far = lax.all_to_all(partial, FAR, 0, 0, tiled=True)]
    all_to_all x2 -> x1, waiting for transfers between devices: 26.2 us -> 10.8 us  [on_device(): weights = lax.all_to_all(copies, NEAR_BACK, 0, 0, tiled=True)]
    all_to_all x2 -> x1, starting transfers between devices: 9.04 us -> 4.6 us  [on_device(): weights = lax.all_to_all(copies, NEAR_BACK, 0, 0, tiled=True)]
    broadcast_in_dim x3 -> x2, local copies, waits for them, and re-layouts: 3.62 us -> 1.05 us  [the longest x1 1.04 us: on_device(): copies = jnp.broadcast_to(block, (n_near, *block.shape))]
    ppermute x0 -> x1, starting transfers between devices: none -> 2.06 us  [on_device(): other = lax.ppermute(normed, 'mp', [(0, 1), (1, 0)])]
    dot_general x1 -> x2, matrix products: 1.72 us -> 3.62 us  [product(): lax.dot_general(rows, cols, (((0,), (0,)), ((), ())), preferred_element_t...]
  transfers between devices with their start and end apart: 2 -> 2, of which waited for: 2 -> 1; matrix products, arithmetic and copies ran while one was open for 1% -> 4% of each run, Pallas kernels for 0% -> 0%
where the time goes in v1:
time: 91.8 us; the launch traced here: 91.4 us
  blocking collectives  63.8 us (69%)
  waiting for transfers between devices  10.8 us (12%)
  starting transfers between devices  6.66 us (7%)
  matrix products  3.62 us (4%)
  other arithmetic  2.68 us (3%)
  local copies, waits for them, and re-layouts  2.38 us (3%)
  between operations  1.44 us (2%)
    all_to_all x1, blocking collectives, on_device(): far = lax.all_to_all(partial, FAR, 0, 0, tiled=True)  24.5 us
    all_to_all x1, blocking collectives, on_device(): near = lax.all_to_all(pieces, NEAR, 0, 0, tiled=True)  23.8 us
    all_to_all x1, blocking collectives, on_device(): lax.all_to_all(copies, FAR_BACK, 0, 0, tiled=True)  15.5 us
    all_to_all x1, waiting for transfers between devices, on_device(): weights = lax.all_to_all(copies, NEAR_BACK, 0, 0, tiled=True)  10.8 us
    all_to_all x1, starting transfers between devices, on_device(): weights = lax.all_to_all(copies, NEAR_BACK, 0, 0, tiled=True)  4.6 us
    dot_general x2, matrix products, product(): lax.dot_general(rows, cols, (((0,), (0,)), ((), ())), preferred_element_t...  3.62 us
    ppermute x1, starting transfers between devices, on_device(): other = lax.ppermute(normed, 'mp', [(0, 1), (1, 0)])  2.06 us
  transfers between devices with their start and end apart: 2, of which 1 were waited for; matrix products, arithmetic and copies ran while one was open for 4% of the time, Pallas kernels for 0%

profile of v1, /device:TPU:8, one launch (start us, length us, event | category | flops | bytes accessed | tf_op | source)
XLA Modules:
  0.0 91.4 jit_solution(6510107062760356761)
XLA Ops:
  0.6 0.0 copy-start
  0.6 0.0 copy-start.1
  0.7 2.1 %collective-permute-start = (bf16[192,2048]{1,0:T(8,128)(2,1)}, bf16[192,2048]{1,0:T(8,128)(2,1)}, u32[]{:S(2)}, u32[]{:S(2)}) collective-permute-start(bf16[192,2048]{1,0:T(8,128)(2,1)} %param.9), channel_id=1, source_target_pairs={{0,1},{1,0},{2,3},{3,2},{4,5},{5,4},{6,7},{7,6},{8,9},{9,8},{10,11... | collective-permute-start | bytes 2359304 | tf_op jit(solution)/shard_map/ppermute | solution.py:43
  3.4 0.7 select_reduce_fusion
  4.1 0.0 copy-done
  4.1 1.7 %fusion.4 = f32[256,2048]{0,1:T(8,128)S(1)} fusion(bf16[192,2048]{1,0:T(8,128)(2,1)} %param.9, bf16[384,256]{1,0:T(8,128)(2,1)S(1)} %copy-done, s32[]{:T(128)S(6)} %select_n.20), kind=kOutput, calls=%fused_computation.10 | convolution fusion | flops 201326592 | bytes 2981892 | tf_op jit(solution)/shard_map/dot_general | solution.py:27
  5.8 0.0 collective-permute-done
  5.8 0.0 copy-done.1
  5.9 1.9 %multiply_convert_fusion = (f16[2048,256]{1,0:T(8,128)(2,1)S(1)}, bf16[2048,256]{1,0:T(8,128)(2,1)S(1)}) fusion(bf16[1,2048,256]{2,1,0:T(8,128)(2,1)S(1)} %copy-done.1, f32[256]{0:T(256)S(1)} %convert_multiply_fusion, f32[256,2048]{0,1:T(8,128)S(1)} %fusion.4, bf16[192,2048]{1,0:T(8,128)(2,1)} %collective-permute-done, bf16[384,256]{1,0:T(8,128)(2,1)S(1)} %copy-done, ...), kind=kOutput, calls=%fused_computation.3 | convolution fusion | flops 204472320 | bytes 6128644 | tf_op jit(solution)/shard_map/dot_general | solution.py:27
  7.8 0.2 copy.18
  8.0 0.0 copy-start.2
  8.1 0.0 copy-start.3
  8.1 0.0 copy-start.4
  8.1 0.0 copy-start.5
  8.1 23.8 %all_to_all.20 = f16[8,256,256]{2,1,0:T(8,128)(2,1)S(1)} all-to-all(f16[8,256,256]{2,1,0:T(8,128)(2,1)S(1)} %bitcast.27), channel_id=1, replica_groups=mesh['zh'=4,'zl'=2,'x'=4,'yh'=4,'yl'=2,'mp'=2] {'x','yl'}, dimensions={0} | all-to-all | bytes 2097152 | tf_op jit(solution)/shard_map/all_to_all | solution.py:58
  31.9 0.1 convert_reduce_fusion
  32.1 24.5 %all_to_all.21 = f16[32,8,256]{2,1,0:T(8,128)(2,1)S(1)} all-to-all(f16[32,8,256]{2,1,0:T(8,128)(2,1)S(1)} %fusion.2), channel_id=1, replica_groups=mesh['zh'=4,'zl'=2,'x'=4,'yh'=4,'yl'=2,'mp'=2] {'zh','zl','yh'}, dimensions={0} | all-to-all | bytes 262144 | tf_op jit(solution)/shard_map/all_to_all | solution.py:61
  56.6 0.0 copy-done.2
  56.6 0.0 copy-done.3
  56.6 0.0 copy-done.4
  56.6 0.0 copy-done.5
  56.6 0.6 fusion.9
  57.3 15.5 %all_to_all.22 = bf16[32,8,256]{2,1,0:T(8,128)(2,1)S(1)} all-to-all(bf16[32,8,256]{2,1,0:T(8,128)(2,1)S(1)} %broadcast_in_dim.21), channel_id=1, replica_groups=mesh['zh'=4,'zl'=2,'x'=4,'yh'=4,'yl'=2,'mp'=2] {'zh','zl','yh'}, dimensions={0} | all-to-all | bytes 262144 | tf_op jit(solution)/shard_map/all_to_all | solution.py:73
  72.8 1.0 %broadcast_in_dim.22 = bf16[8,256,256]{2,1,0:T(8,128)(2,1)} broadcast(bf16[256,256]{1,0:T(8,128)(2,1)S(1)} %bitcast.30), dimensions={1,2} | broadcast | bytes 1179648 | tf_op jit(solution)/shard_map/broadcast_in_dim | solution.py:74
  73.8 4.6 %all-to-all-start.3 = ((bf16[8,256,256]{2,1,0:T(8,128)(2,1)}), bf16[8,256,256]{2,1,0:T(8,128)(2,1)S(1)}, u32[]{:S(2)}, u32[]{:S(2)}) async-start(bf16[8,256,256]{2,1,0:T(8,128)(2,1)} %broadcast_in_dim.22), calls=%async_computation.3 | async-start | bytes 2097152 | tf_op jit(solution)/shard_map/all_to_all | solution.py:75
  78.5 1.1 %fusion.1 = bf16[1,2048,256]{2,1,0:T(8,128)(2,1)} fusion(bf16[1,2048,256]{2,1,0:T(8,128)(2,1)S(1)} %copy-done.1, bf16[2048,256]{1,0:T(8,128)(2,1)S(1)} %get-tuple-element.12, pred[256]{0:T(512)(128)(4,1)S(1)} %multiply_compare_fusion), kind=kLoop, calls=%fused_computation.5 | loop fusion | flops 524288 | bytes 3145984 | tf_op jit(solution)/shard_map/broadcast_in_dim | solution.py:81
  79.5 10.8 %all-to-all-done.3 = bf16[8,256,256]{2,1,0:T(8,128)(2,1)S(1)} async-done(((bf16[8,256,256]{2,1,0:T(8,128)(2,1)}), bf16[8,256,256]{2,1,0:T(8,128)(2,1)S(1)}, u32[]{:S(2)}, u32[]{:S(2)}) %all-to-all-start.3) | async-done | bytes 1048608 | tf_op jit(solution)/shard_map/all_to_all | solution.py:75
  90.4 1.1 %copy.19 = bf16[4,2,4,4,2,8,256]{6,5,4,3,2,1,0:T(8,128)(2,1)} copy(bf16[4,2,4,4,2,8,256]{6,5,3,1,0,4,2:T(8,128)(2,1)S(1)} %bitcast.26) | data formatting | bytes 2097152 | tf_op jit(solution)/shard_map/transpose | solution.py:78
  (6 shorter events, 0.1 us)
Async XLA Ops:
  0.6 3.5 %copy-start = (bf16[384,256]{1,0:T(8,128)(2,1)S(1)}, bf16[384,256]{1,0:T(8,128)(2,1)}, u32[]{:S(2)}) copy-start(bf16[384,256]{1,0:T(8,128)(2,1)} %param.10) | copy-start | bytes 589828
  0.6 5.2 %copy-start.1 = (bf16[1,2048,256]{2,1,0:T(8,128)(2,1)S(1)}, bf16[1,2048,256]{2,1,0:T(8,128)(2,1)}, u32[]{:S(2)}) copy-start(bf16[1,2048,256]{2,1,0:T(8,128)(2,1)} %param.11) | copy-start | bytes 3145732
  0.7 5.2 %collective-permute-start = (bf16[192,2048]{1,0:T(8,128)(2,1)}, bf16[192,2048]{1,0:T(8,128)(2,1)}, u32[]{:S(2)}, u32[]{:S(2)}) collective-permute-start(bf16[192,2048]{1,0:T(8,128)(2,1)} %param.9), channel_id=1, source_target_pairs={{0,1},{1,0},{2,3},{3,2},{4,5},{5,4},{6,7},{7,6},{8,9},{9,8},{10,11... | collective-permute-start | bytes 2359304 | tf_op jit(solution)/shard_map/ppermute | solution.py:43
  8.0 48.6 %copy-start.2 = (f32[8,256]{1,0:T(8,128)S(1)}, f32[8,256]{1,0:T(8,128)}, u32[]{:S(2)}) copy-start(f32[8,256]{1,0:T(8,128)} %param.15) | copy-start | bytes 24580
  8.1 48.6 %copy-start.3 = (f32[8,256]{1,0:T(8,128)S(1)}, f32[8,256]{1,0:T(8,128)}, u32[]{:S(2)}) copy-start(f32[8,256]{1,0:T(8,128)} %param.16) | copy-start | bytes 24580
  8.1 48.6 %copy-start.4 = (f32[8,256]{1,0:T(8,128)S(1)}, f32[8,256]{1,0:T(8,128)}, u32[]{:S(2)}) copy-start(f32[8,256]{1,0:T(8,128)} %param.17) | copy-start | bytes 24580
  8.1 48.6 %copy-start.5 = (f32[8,256]{1,0:T(8,128)S(1)}, f32[8,256]{1,0:T(8,128)}, u32[]{:S(2)}) copy-start(f32[8,256]{1,0:T(8,128)} %param.14) | copy-start | bytes 24580
  73.8 16.5 %all-to-all-start.3 = ((bf16[8,256,256]{2,1,0:T(8,128)(2,1)}), bf16[8,256,256]{2,1,0:T(8,128)(2,1)S(1)}, u32[]{:S(2)}, u32[]{:S(2)}) async-start(bf16[8,256,256]{2,1,0:T(8,128)(2,1)} %broadcast_in_dim.22), calls=%async_computation.3 | async-start | bytes 2097152 | tf_op jit(solution)/shard_map/all_to_all | solution.py:75

commit v2 on v1

v2 whole, which is shorter than its diff:
```python
import functools

import jax
import jax.numpy as jnp
from jax import lax
from jax.experimental import pallas as pl
from jax.experimental.pallas import tpu as pltpu
from jax.sharding import Mesh
from jax.sharding import PartitionSpec as P

H = 512
BLOCKS = 4
STEP = 10
DP = ("z", "x", "yh", "yl")
NEAR = ("x", "yl")
FAR = ("z", "yh")
SCALE_ONE = 256.0
SCALE_TWO = 32.0
VMEM_LIMIT = 16 * 2**20

beta_one = 0.9
beta_two = 0.95
learn_rate = 0.001
decay_rate = 0.1
epsilon = 1e-08


def dot_over_tokens(rows, cols):
    return lax.dot_general(rows, cols, (((0,), (0,)), ((), ())), preferred_element_type=jnp.float32)


def own_half_kernel(
    flag_ref, mask_ref, normed_ref, cols_ref, stale_ref, part_ref, other_cols_ref, old_ref, fired_ref,
    own, cols, mask, sems
):
    core = lax.axis_index("mp")
    tokens, half_cols = own.shape[0], cols.shape[1]
    copies = [
        pltpu.make_async_copy(cols_ref, cols, sems.at[0]),
        pltpu.make_async_copy(normed_ref, own, sems.at[1]),
        pltpu.make_async_copy(mask_ref, mask, sems.at[2]),
        pltpu.make_async_copy(stale_ref, old_ref, sems.at[3]),
    ]
    for copy in copies:
        copy.start()
    copies[0].wait()
    own_cols = cols[pl.ds(pl.multiple_of(core * tokens, tokens), tokens), :]
    other_cols_ref[...] = cols[pl.ds(pl.multiple_of((1 - core) * tokens, tokens), tokens), :]
    copies[1].wait()
    step = 256
    for at in range(0, own.shape[1], step):
        part_ref[at : at + step, :] = dot_over_tokens(own[:, at : at + step], own_cols)
    copies[2].wait()
    width = H // BLOCKS
    column = lax.broadcasted_iota(jnp.int32, (1, half_cols), 1) + core * half_cols
    fired = jnp.zeros((1, half_cols), jnp.int32)
    for b in range(BLOCKS):
        inside = (column >= b * width) & (column < (b + 1) * width)
        fired = fired + jnp.where(inside, flag_ref[0] * mask[0, b], 0)
    fired_ref[...] = fired.astype(jnp.float32)
    copies[3].wait()


def gradient_kernel(
    sizes, part_ref, other_ref, cols_ref, old_ref, fired_ref, term_ref, kept_ref
):
    nz, nx, nh, nl = sizes
    own_rows = term_ref.shape[1]
    block = nx * nh * nl * own_rows
    fired = fired_ref[...]
    weight = fired * SCALE_ONE
    cols = cols_ref[...]
    for z in range(nz):
        span = slice(z * block, (z + 1) * block)
        grad = part_ref[span, :] + dot_over_tokens(other_ref[:, span], cols)
        old = old_ref[span, :]
        kept_ref[span, :] = jnp.where(fired > 0, grad.astype(jnp.bfloat16), old)
        term = weight * (grad - old.astype(jnp.float32))
        for x in range(nx):
            for yh in range(nh):
                for yl in range(nl):
                    at = ((x * nh + yh) * nl + yl) * own_rows
                    term_ref[((x * nl + yl) * nz + z) * nh + yh] = term[at : at + own_rows, :]


def store_kernel(n_rest, weights_ref, *refs):
    rest, (out_ref, *outs, sems) = refs[:n_rest], refs[n_rest:]
    _, nx, _, nl, _, _ = out_ref.shape
    copies = []
    for x in range(nx):
        for yl in range(nl):
            n = x * nl + yl
            copies.append(
                pltpu.make_async_copy(weights_ref.at[n], out_ref.at[:, x, :, yl], sems.at[n])
            )
    for i in range(n_rest):
        copies.append(pltpu.make_async_copy(rest[i], outs[i], sems.at[nx * nl + i]))
    for copy in copies:
        copy.start()
    for copy in copies:
        copy.wait()


def on_device(
    normed, key_grad, stale, worker_flag, block_mask, aggregate, master, moment_one, moment_two
):
    rows, half_cols = normed.shape[0], key_grad.shape[1]
    d = normed.shape[1]
    other = lax.ppermute(normed, "mp", [(0, 1), (1, 0)])
    sizes = tuple(lax.axis_size(a) for a in DP)
    n_near, n_far = lax.axis_size(NEAR), lax.axis_size(FAR)
    own = d // (n_near * n_far)
    smem = pl.BlockSpec(memory_space=pltpu.SMEM)
    vmem = pl.BlockSpec(memory_space=pltpu.VMEM)
    hbm = pl.BlockSpec(memory_space=pltpu.HBM)
    params = pltpu.CompilerParams(vmem_limit_bytes=VMEM_LIMIT)
    part, other_cols, old, fired = pl.pallas_call(
        own_half_kernel,
        out_shape=(
            jax.ShapeDtypeStruct((d, half_cols), jnp.float32),
            jax.ShapeDtypeStruct((rows, half_cols), jnp.bfloat16),
            jax.ShapeDtypeStruct((d, half_cols), jnp.bfloat16),
            jax.ShapeDtypeStruct((1, half_cols), jnp.float32),
        ),
        in_specs=[smem] + [hbm] * 4,
        out_specs=(vmem,) * 4,
        scratch_shapes=[
            pltpu.VMEM(normed.shape, normed.dtype),
            pltpu.VMEM(key_grad.shape, key_grad.dtype),
            pltpu.SMEM(block_mask.shape, block_mask.dtype),
            pltpu.SemaphoreType.DMA((4,)),
        ],
        compiler_params=params,
    )(
        worker_flag,
        *(
            pltpu.with_memory_space_constraint(a, pltpu.HBM)
            for a in (block_mask, normed, key_grad, stale[0])
        )
    )
    term, kept = pl.pallas_call(
        functools.partial(gradient_kernel, sizes),
        out_shape=(
            jax.ShapeDtypeStruct((d // own, own, half_cols), jnp.float32),
            jax.ShapeDtypeStruct((d, half_cols), jnp.bfloat16),
        ),
        in_specs=[vmem] * 5,
        out_specs=(vmem, vmem),
        compiler_params=params,
    )(part, other, other_cols, old, fired)
    pieces = term.astype(jnp.float16).reshape(n_near, n_far * own, half_cols)
    near = lax.all_to_all(pieces, NEAR, 0, 0, tiled=True)
    partial = jnp.sum(near.astype(jnp.float32), axis=0) * (SCALE_TWO / SCALE_ONE)
    partial = partial.astype(jnp.float16).reshape(n_far, own, half_cols)
    far = lax.all_to_all(partial, FAR, 0, 0, tiled=True)
    reduced = jnp.sum(far.astype(jnp.float32), axis=0) * (1.0 / SCALE_TWO)
    new_aggregate = aggregate + reduced
    new_moment_one = beta_one * moment_one + (1.0 - beta_one) * new_aggregate
    new_moment_two = beta_two * moment_two + (1.0 - beta_two) * new_aggregate * new_aggregate
    first_hat = new_moment_one / (1.0 - beta_one**STEP)
    second_hat = new_moment_two / (1.0 - beta_two**STEP)
    update = first_hat / (jnp.sqrt(second_hat) + epsilon)
    new_master = master - learn_rate * (update + decay_rate * master)
    fresh = new_master.astype(jnp.bfloat16)
    copies = jnp.broadcast_to(fresh, (n_far, own, half_cols))
    block = lax.all_to_all(copies, FAR, 0, 0, tiled=True).reshape(n_far * own, half_cols)
    copies = jnp.broadcast_to(block, (n_near, *block.shape))
    weights = lax.all_to_all(copies, NEAR, 0, 0, tiled=True)
    weights = weights.reshape(n_near, sizes[0], sizes[2], own, half_cols)
    rest = (new_aggregate, new_master, new_moment_one, new_moment_two, kept)
    weights, *rest = pl.pallas_call(
        functools.partial(store_kernel, len(rest)),
        out_shape=(
            jax.ShapeDtypeStruct((*sizes, own, half_cols), jnp.bfloat16),
            *(jax.ShapeDtypeStruct(a.shape, a.dtype) for a in rest),
        ),
        in_specs=[vmem] * (1 + len(rest)),
        out_specs=(hbm,) * (1 + len(rest)),
        scratch_shapes=[pltpu.SemaphoreType.DMA((n_near + len(rest),))],
        compiler_params=params,
    )(weights, *rest)
    return (*rest[:4], weights.reshape(d, half_cols), rest[4][None])


def solution(mesh):
    torus = Mesh(mesh.devices.reshape(8, 4, 4, 2, mesh.shape["mp"]), (*DP, "mp"))
    return jax.shard_map(
        on_device,
        mesh=torus,
        in_specs=(
            P((*DP, "mp"), None),
            P(DP, "mp"),
            P(DP, None, "mp"),
            P(DP),
            P(DP, None),
            P(DP, "mp"),
            P(DP, "mp"),
            P(DP, "mp"),
            P(DP, "mp"),
        ),
        out_specs=(
            P(DP, "mp"),
            P(DP, "mp"),
            P(DP, "mp"),
            P(DP, "mp"),
            P(None, "mp"),
            P(DP, None, "mp"),
        ),
        check_vma=False,
    )
```

time: 91.8 us -> 87.4 us (0.952)
  blocking collectives: 63.8 us -> 79.3 us
  waiting for transfers between devices: 10.8 us -> 0.01 us
  starting transfers between devices: 6.66 us -> 1.92 us
  Pallas kernels: 0 us -> 3.93 us
  matrix products: 3.62 us -> 0 us
  local copies, waits for them, and re-layouts: 2.38 us -> 0.1 us
  other arithmetic: 2.68 us -> 0.43 us
    all_to_all x1 -> x2, blocking collectives: 15.5 us -> 31 us  [the longest x1 15.5 us: on_device(): lax.all_to_all(copies, FAR, 0, 0, tiled=True)]
    all_to_all x1 -> x0, waiting for transfers between devices: 10.8 us -> none  [on_device(): weights = lax.all_to_all(copies, NEAR_BACK, 0, 0, tiled=True)]
    all_to_all x1 -> x0, starting transfers between devices: 4.6 us -> none  [on_device(): weights = lax.all_to_all(copies, NEAR_BACK, 0, 0, tiled=True)]
    pallas_call x0 -> x3, Pallas kernels: none -> 3.93 us  [the longest x1 1.8 us: on_device(): pl.pallas_call(own_half_kernel, out_shape=(jax.ShapeDtypeStruct((d, half_...]
    dot_general x2 -> x0, matrix products: 3.62 us -> none  [product(): lax.dot_general(rows, cols, (((0,), (0,)), ((), ())), preferred_element_t...]
    broadcast_in_dim x1 -> x0, other arithmetic: 1.08 us -> none  [on_device(): kept[None]]
    transpose x1 -> x0, local copies, waits for them, and re-layouts: 1.05 us -> none  [on_device(): weights.transpose(*(back.index(a) for a in DP), len(DP), len(DP) + 1)]
    broadcast_in_dim x1, local copies, waits for them, and re-layouts: 1.04 us -> 0.07 us  [on_device(): copies = jnp.broadcast_to(block, (n_near, *block.shape))]
  transfers between devices with their start and end apart: 2 -> 1, of which waited for: 1 -> 0; matrix products, arithmetic and copies ran while one was open for 4% -> 0% of each run, Pallas kernels for 0% -> 2%
where the time goes in v2:
time: 87.4 us; the launch traced here: 87.1 us
  blocking collectives  79.3 us (91%)
  Pallas kernels  3.93 us (4%)
  starting transfers between devices  1.92 us (2%)
  between operations  1.4 us (2%)
    all_to_all x1, blocking collectives, on_device(): far = lax.all_to_all(partial, FAR, 0, 0, tiled=True)  24.5 us
    all_to_all x1, blocking collectives, on_device(): near = lax.all_to_all(pieces, NEAR, 0, 0, tiled=True)  23.8 us
    all_to_all x1, blocking collectives, on_device(): lax.all_to_all(copies, FAR, 0, 0, tiled=True)  15.5 us
    all_to_all x1, blocking collectives, on_device(): weights = lax.all_to_all(copies, NEAR, 0, 0, tiled=True)  15.4 us
    ppermute x1, starting transfers between devices, on_device(): other = lax.ppermute(normed, 'mp', [(0, 1), (1, 0)])  1.92 us
    pallas_call x1, Pallas kernels, on_device(): pl.pallas_call(own_half_kernel, out_shape=(jax.ShapeDtypeStruct((d, half_...  1.8 us
  transfers between devices with their start and end apart: 1, of which 0 were waited for; matrix products, arithmetic and copies ran while one was open for 0% of the time, Pallas kernels for 2%

profile of v2, /device:TPU:8, one launch (start us, length us, event | category | flops | bytes accessed | tf_op | source)
XLA Modules:
  0.0 87.1 jit_solution(13073088358584862637)
XLA Ops:
  0.6 1.9 %collective-permute-start = (bf16[192,2048]{1,0:T(8,128)(2,1)}, bf16[192,2048]{1,0:T(8,128)(2,1)S(1)}, u32[]{:S(2)}, u32[]{:S(2)}) collective-permute-start(bf16[192,2048]{1,0:T(8,128)(2,1)} %normed_ref.1), channel_id=1, source_target_pairs={{0,1},{1,0},{2,3},{3,2},{4,5},{5,4},{6,7},{7,6},{8,9},{9,8},{10,11... | collective-permute-start | bytes 2359304 | tf_op jit(solution)/shard_map/ppermute | solution.py:109
  3.2 1.8 %shard_map.136 = (f32[2048,256]{1,0:T(8,128)S(1)}, bf16[192,256]{1,0:T(8,128)(2,1)S(1)}, bf16[2048,256]{1,0:T(8,128)(2,1)S(1)}, f32[1,256]{1,0:T(1,128)S(1)}) custom-call(s32[1]{0:T(128)S(6)} %copy.15.flag_ref, s32[1,4]{1,0:T(1,128)} %mask_ref.1, bf16[192,2048]{1,0:T(8,128)(2,1)} %normed_ref.1, bf16[384,256]{1,0:T(8,128)(2,1)} %cols_ref.1, ...), custom_call_target="tpu_custom_call" | custom-call | tf_op jit(solution)/shard_map/pallas_call | solution.py:117
  5.0 0.0 collective-permute-done.other_ref
  5.0 0.7 shard_map.137
  5.7 0.2 convert_element_type.19
  5.9 0.0 copy-start
  5.9 0.0 copy-start.1
  6.0 0.0 copy-start.2
  6.0 0.0 copy-start.3
  6.0 23.8 %all_to_all.20 = f16[8,256,256]{2,1,0:T(8,128)(2,1)S(1)} all-to-all(f16[8,256,256]{2,1,0:T(8,128)(2,1)S(1)} %bitcast.9), channel_id=1, replica_groups=mesh['z'=8,'x'=4,'yh'=4,'yl'=2,'mp'=2] {'x','yl'}, dimensions={0} | all-to-all | bytes 2097152 | tf_op jit(solution)/shard_map/all_to_all | solution.py:152
  29.8 0.1 convert_reduce_fusion
  30.0 24.5 %all_to_all.21 = f16[32,8,256]{2,1,0:T(8,128)(2,1)S(1)} all-to-all(f16[32,8,256]{2,1,0:T(8,128)(2,1)S(1)} %fusion), channel_id=1, replica_groups=mesh['z'=8,'x'=4,'yh'=4,'yl'=2,'mp'=2] {'z','yh'}, dimensions={0} | all-to-all | bytes 262144 | tf_op jit(solution)/shard_map/all_to_all | solution.py:155
  54.5 0.0 copy-done
  54.5 0.0 copy-done.1
  54.5 0.0 copy-done.2
  54.5 0.0 copy-done.3
  54.6 15.5 %all_to_all.22 = bf16[32,8,256]{2,1,0:T(8,128)(2,1)S(1)} all-to-all(bf16[32,8,256]{2,1,0:T(8,128)(2,1)S(1)} %broadcast_in_dim.9), channel_id=1, replica_groups=mesh['z'=8,'x'=4,'yh'=4,'yl'=2,'mp'=2] {'z','yh'}, dimensions={0} | all-to-all | bytes 262144 | tf_op jit(solution)/shard_map/all_to_all | solution.py:166
  70.1 0.1 broadcast_in_dim.10
  70.2 15.4 %all_to_all.23 = bf16[8,256,256]{2,1,0:T(8,128)(2,1)S(1)} all-to-all(bf16[8,256,256]{2,1,0:T(8,128)(2,1)S(1)} %broadcast_in_dim.10), channel_id=1, replica_groups=mesh['z'=8,'x'=4,'yh'=4,'yl'=2,'mp'=2] {'x','yl'}, dimensions={0} | all-to-all | bytes 2097152 | tf_op jit(solution)/shard_map/all_to_all | solution.py:168
  85.6 1.4 %shard_map.138 = (bf16[8,4,4,2,8,256]{5,4,3,2,1,0:T(8,128)(2,1)}, f32[8,256]{1,0:T(8,128)}, f32[8,256]{1,0:T(8,128)}, f32[8,256]{1,0:T(8,128)}, f32[8,256]{1,0:T(8,128)}, /*index=5*/bf16[2048,256]{1,0:T(8,128)(2,1)}) custom-call(bf16[8,8,4,8,256]{4,3,2,1,0:T(8,128)(2,1)S(1)} %bitcast.8, f32[8,256]{1,0:T(8,128)S(1)} %get-tuple-element.34.refs_0_, ...), custom_call_target="tpu_custom_call" | custom-call | tf_op jit(solution)/shard_map/pallas_call | solution.py:171
  (4 shorter events, 0.1 us)
Async XLA Ops:
  0.6 4.4 %collective-permute-start = (bf16[192,2048]{1,0:T(8,128)(2,1)}, bf16[192,2048]{1,0:T(8,128)(2,1)S(1)}, u32[]{:S(2)}, u32[]{:S(2)}) collective-permute-start(bf16[192,2048]{1,0:T(8,128)(2,1)} %normed_ref.1), channel_id=1, source_target_pairs={{0,1},{1,0},{2,3},{3,2},{4,5},{5,4},{6,7},{7,6},{8,9},{9,8},{10,11... | collective-permute-start | bytes 2359304 | tf_op jit(solution)/shard_map/ppermute | solution.py:109
  5.9 48.6 %copy-start = (f32[8,256]{1,0:T(8,128)S(1)}, f32[8,256]{1,0:T(8,128)}, u32[]{:S(2)}) copy-start(f32[8,256]{1,0:T(8,128)} %param.15) | copy-start | bytes 24580
  5.9 48.6 %copy-start.1 = (f32[8,256]{1,0:T(8,128)S(1)}, f32[8,256]{1,0:T(8,128)}, u32[]{:S(2)}) copy-start(f32[8,256]{1,0:T(8,128)} %param.16) | copy-start | bytes 24580
  6.0 48.6 %copy-start.2 = (f32[8,256]{1,0:T(8,128)S(1)}, f32[8,256]{1,0:T(8,128)}, u32[]{:S(2)}) copy-start(f32[8,256]{1,0:T(8,128)} %param.17) | copy-start | bytes 24580
  6.0 48.6 %copy-start.3 = (f32[8,256]{1,0:T(8,128)S(1)}, f32[8,256]{1,0:T(8,128)}, u32[]{:S(2)}) copy-start(f32[8,256]{1,0:T(8,128)} %param.14) | copy-start | bytes 24580

commit v3 on v2

--- a/solution.py
+++ b/solution.py
@@ -17,6 +17,7 @@
 SCALE_ONE = 256.0
 SCALE_TWO = 32.0
 VMEM_LIMIT = 16 * 2**20
+LATER_NS = 1000
 
 beta_one = 0.9
 beta_two = 0.95
@@ -62,7 +63,7 @@
 
 
 def gradient_kernel(
-    sizes, part_ref, other_ref, cols_ref, old_ref, fired_ref, term_ref, kept_ref
+    sizes, part_ref, other_ref, cols_ref, old_ref, fired_ref, term_ref, kept_ref, stored_ref, sem
 ):
     nz, nx, nh, nl = sizes
     own_rows = term_ref.shape[1]
@@ -82,9 +83,18 @@
                     at = ((x * nh + yh) * nl + yl) * own_rows
                     term_ref[((x * nl + yl) * nz + z) * nh + yh] = term[at : at + own_rows, :]
 
-
-def store_kernel(n_rest, weights_ref, *refs):
-    rest, (out_ref, *outs, sems) = refs[:n_rest], refs[n_rest:]
+    @pl.when(lax.axis_index("mp") == 0)
+    def _():
+        copy = pltpu.make_async_copy(kept_ref, stored_ref, sem)
+        copy.start()
+        copy.wait()
+        if LATER_NS:
+            pl.delay(LATER_NS)
+
+
+def store_kernel(n_rest, weights_ref, kept_ref, stored_ref, *refs):
+    del stored_ref
+    rest, (out_ref, stale_ref, *outs, sems) = refs[:n_rest], refs[n_rest:]
     _, nx, _, nl, _, _ = out_ref.shape
     copies = []
     for x in range(nx):
@@ -97,6 +107,13 @@
         copies.append(pltpu.make_async_copy(rest[i], outs[i], sems.at[nx * nl + i]))
     for copy in copies:
         copy.start()
+
+    @pl.when(lax.axis_index("mp") != 0)
+    def _():
+        copy = pltpu.make_async_copy(kept_ref, stale_ref, sems.at[nx * nl + n_rest])
+        copy.start()
+        copy.wait()
+
     for copy in copies:
         copy.wait()
 
@@ -138,14 +155,16 @@
             for a in (block_mask, normed, key_grad, stale[0])
         )
     )
-    term, kept = pl.pallas_call(
+    term, kept, stored = pl.pallas_call(
         functools.partial(gradient_kernel, sizes),
         out_shape=(
             jax.ShapeDtypeStruct((d // own, own, half_cols), jnp.float32),
             jax.ShapeDtypeStruct((d, half_cols), jnp.bfloat16),
+            pltpu.HBM((d, half_cols), jnp.bfloat16),
         ),
         in_specs=[vmem] * 5,
-        out_specs=(vmem, vmem),
+        out_specs=(vmem, vmem, hbm),
+        scratch_shapes=[pltpu.SemaphoreType.DMA(())],
         compiler_params=params,
     )(part, other, other_cols, old, fired)
     pieces = term.astype(jnp.float16).reshape(n_near, n_far * own, half_cols)
@@ -167,19 +186,21 @@
     copies = jnp.broadcast_to(block, (n_near, *block.shape))
     weights = lax.all_to_all(copies, NEAR, 0, 0, tiled=True)
     weights = weights.reshape(n_near, sizes[0], sizes[2], own, half_cols)
-    rest = (new_aggregate, new_master, new_moment_one, new_moment_two, kept)
-    weights, *rest = pl.pallas_call(
+    rest = (new_aggregate, new_master, new_moment_one, new_moment_two)
+    weights, new_stale, *rest = pl.pallas_call(
         functools.partial(store_kernel, len(rest)),
         out_shape=(
             jax.ShapeDtypeStruct((*sizes, own, half_cols), jnp.bfloat16),
+            pltpu.HBM(kept.shape, kept.dtype),
             *(jax.ShapeDtypeStruct(a.shape, a.dtype) for a in rest),
         ),
-        in_specs=[vmem] * (1 + len(rest)),
-        out_specs=(hbm,) * (1 + len(rest)),
-        scratch_shapes=[pltpu.SemaphoreType.DMA((n_near + len(rest),))],
+        in_specs=[vmem, vmem, hbm] + [vmem] * len(rest),
+        out_specs=(hbm,) * (2 + len(rest)),
+        input_output_aliases={2: 1},
+        scratch_shapes=[pltpu.SemaphoreType.DMA((n_near + len(rest) + 1,))],
         compiler_params=params,
-    )(weights, *rest)
-    return (*rest[:4], weights.reshape(d, half_cols), rest[4][None])
+    )(weights, kept, stored, *rest)
+    return (*rest, weights.reshape(d, half_cols), new_stale[None])
 
 
 def solution(mesh):

time: 87.4 us -> 85.6 us (0.979)
  blocking collectives: 79.3 us -> 75.8 us
  Pallas kernels: 3.93 us -> 5.55 us
    pallas_call x1, Pallas kernels: 0.69 us -> 2.67 us  [on_device(): pl.pallas_call(functools.partial(gradient_kernel, sizes), out_shape=(jax....]
    all_to_all x1, blocking collectives: 23.8 us -> 21.9 us  [on_device(): near = lax.all_to_all(pieces, NEAR, 0, 0, tiled=True)]
    all_to_all x1, blocking collectives: 15.4 us -> 14 us  [on_device(): weights = lax.all_to_all(copies, NEAR, 0, 0, tiled=True)]
where the time goes in v3:
time: 85.6 us; the launch traced here: 85.3 us
  blocking collectives  75.8 us (89%)
  Pallas kernels  5.55 us (6%)
  starting transfers between devices  1.92 us (2%)
  between operations  1.4 us (2%)
    all_to_all x1, blocking collectives, on_device(): far = lax.all_to_all(partial, FAR, 0, 0, tiled=True)  24.4 us
    all_to_all x1, blocking collectives, on_device(): near = lax.all_to_all(pieces, NEAR, 0, 0, tiled=True)  21.9 us
    all_to_all x1, blocking collectives, on_device(): lax.all_to_all(copies, FAR, 0, 0, tiled=True)  15.6 us
    all_to_all x1, blocking collectives, on_device(): weights = lax.all_to_all(copies, NEAR, 0, 0, tiled=True)  14 us
    pallas_call x1, Pallas kernels, on_device(): pl.pallas_call(functools.partial(gradient_kernel, sizes), out_shape=(jax....  2.67 us
    ppermute x1, starting transfers between devices, on_device(): other = lax.ppermute(normed, 'mp', [(0, 1), (1, 0)])  1.92 us
    pallas_call x1, Pallas kernels, on_device(): pl.pallas_call(own_half_kernel, out_shape=(jax.ShapeDtypeStruct((d, half_...  1.8 us
  transfers between devices with their start and end apart: 1, of which 0 were waited for; matrix products, arithmetic and copies ran while one was open for 0% of the time, Pallas kernels for 2%

profile of v3, /device:TPU:8, one launch (start us, length us, event | category | flops | bytes accessed | tf_op | source)
XLA Modules:
  0.0 85.3 jit_solution(16433509377655681200)
XLA Ops:
  0.6 1.9 %collective-permute-start = (bf16[192,2048]{1,0:T(8,128)(2,1)}, bf16[192,2048]{1,0:T(8,128)(2,1)S(1)}, u32[]{:S(2)}, u32[]{:S(2)}) collective-permute-start(bf16[192,2048]{1,0:T(8,128)(2,1)} %normed_ref.1), channel_id=1, source_target_pairs={{0,1},{1,0},{2,3},{3,2},{4,5},{5,4},{6,7},{7,6},{8,9},{9,8},{10,11... | collective-permute-start | bytes 2359304 | tf_op jit(solution)/shard_map/ppermute | solution.py:126
  3.2 1.8 %shard_map.136 = (f32[2048,256]{1,0:T(8,128)S(1)}, bf16[192,256]{1,0:T(8,128)(2,1)S(1)}, bf16[2048,256]{1,0:T(8,128)(2,1)S(1)}, f32[1,256]{1,0:T(1,128)S(1)}) custom-call(s32[1]{0:T(128)S(6)} %copy.17.flag_ref, s32[1,4]{1,0:T(1,128)} %mask_ref.1, bf16[192,2048]{1,0:T(8,128)(2,1)} %normed_ref.1, bf16[384,256]{1,0:T(8,128)(2,1)} %cols_ref.1, ...), custom_call_target="tpu_custom_call" | custom-call | tf_op jit(solution)/shard_map/pallas_call | solution.py:134
  5.0 0.0 collective-permute-done.other_ref
  5.0 2.7 %shard_map.137 = (f32[256,8,256]{2,1,0:T(8,128)S(1)}, bf16[2048,256]{1,0:T(8,128)(2,1)S(1)}, bf16[2048,256]{1,0:T(8,128)(2,1)}) custom-call(f32[2048,256]{1,0:T(8,128)S(1)} %get-tuple-element.19.part_ref, bf16[192,2048]{1,0:T(8,128)(2,1)S(1)} %collective-permute-done.other_ref, bf16[192,256]{1,0:T(8,128)(2,1)S(1)} %get-tuple-element.20.cols_ref, ...), custom_call_target="tpu_custom_call" | custom-call | tf_op jit(solution)/shard_map/pallas_call | solution.py:158
  7.7 0.2 convert_element_type.19
  7.9 0.0 copy-start
  7.9 0.0 copy-start.1
  7.9 0.0 copy-start.2
  7.9 0.0 copy-start.3
  8.0 21.9 %all_to_all.20 = f16[8,256,256]{2,1,0:T(8,128)(2,1)S(1)} all-to-all(f16[8,256,256]{2,1,0:T(8,128)(2,1)S(1)} %bitcast.9), channel_id=1, replica_groups=mesh['z'=8,'x'=4,'yh'=4,'yl'=2,'mp'=2] {'x','yl'}, dimensions={0} | all-to-all | bytes 2097152 | tf_op jit(solution)/shard_map/all_to_all | solution.py:171
  29.8 0.1 convert_reduce_fusion
  30.0 24.4 %all_to_all.21 = f16[32,8,256]{2,1,0:T(8,128)(2,1)S(1)} all-to-all(f16[32,8,256]{2,1,0:T(8,128)(2,1)S(1)} %fusion), channel_id=1, replica_groups=mesh['z'=8,'x'=4,'yh'=4,'yl'=2,'mp'=2] {'z','yh'}, dimensions={0} | all-to-all | bytes 262144 | tf_op jit(solution)/shard_map/all_to_all | solution.py:174
  54.5 0.0 copy-done
  54.5 0.0 copy-done.1
  54.5 0.0 copy-done.2
  54.5 0.0 copy-done.3
  54.6 15.6 %all_to_all.22 = bf16[32,8,256]{2,1,0:T(8,128)(2,1)S(1)} all-to-all(bf16[32,8,256]{2,1,0:T(8,128)(2,1)S(1)} %broadcast_in_dim.9), channel_id=1, replica_groups=mesh['z'=8,'x'=4,'yh'=4,'yl'=2,'mp'=2] {'z','yh'}, dimensions={0} | all-to-all | bytes 262144 | tf_op jit(solution)/shard_map/all_to_all | solution.py:185
  70.1 0.1 broadcast_in_dim.10
  70.2 14.0 %all_to_all.23 = bf16[8,256,256]{2,1,0:T(8,128)(2,1)S(1)} all-to-all(bf16[8,256,256]{2,1,0:T(8,128)(2,1)S(1)} %broadcast_in_dim.10), channel_id=1, replica_groups=mesh['z'=8,'x'=4,'yh'=4,'yl'=2,'mp'=2] {'x','yl'}, dimensions={0} | all-to-all | bytes 2097152 | tf_op jit(solution)/shard_map/all_to_all | solution.py:187
  84.2 1.1 %shard_map.138 = (bf16[8,4,4,2,8,256]{5,4,3,2,1,0:T(8,128)(2,1)}, bf16[2048,256]{1,0:T(8,128)(2,1)}, f32[8,256]{1,0:T(8,128)}, f32[8,256]{1,0:T(8,128)}, f32[8,256]{1,0:T(8,128)}, /*index=5*/f32[8,256]{1,0:T(8,128)}) custom-call(bf16[8,8,4,8,256]{4,3,2,1,0:T(8,128)(2,1)S(1)} %bitcast.8, ...), custom_call_target="tpu_custom_call", output_to_operand_aliasing={{1}: (2, {})} | custom-call | tf_op jit(solution)/shard_map/pallas_call | solution.py:190
  (4 shorter events, 0.1 us)
Async XLA Ops:
  0.6 4.4 %collective-permute-start = (bf16[192,2048]{1,0:T(8,128)(2,1)}, bf16[192,2048]{1,0:T(8,128)(2,1)S(1)}, u32[]{:S(2)}, u32[]{:S(2)}) collective-permute-start(bf16[192,2048]{1,0:T(8,128)(2,1)} %normed_ref.1), channel_id=1, source_target_pairs={{0,1},{1,0},{2,3},{3,2},{4,5},{5,4},{6,7},{7,6},{8,9},{9,8},{10,11... | collective-permute-start | bytes 2359304 | tf_op jit(solution)/shard_map/ppermute | solution.py:126
  7.9 46.6 %copy-start = (f32[8,256]{1,0:T(8,128)S(1)}, f32[8,256]{1,0:T(8,128)}, u32[]{:S(2)}) copy-start(f32[8,256]{1,0:T(8,128)} %param.15) | copy-start | bytes 24580
  7.9 46.5 %copy-start.1 = (f32[8,256]{1,0:T(8,128)S(1)}, f32[8,256]{1,0:T(8,128)}, u32[]{:S(2)}) copy-start(f32[8,256]{1,0:T(8,128)} %param.16) | copy-start | bytes 24580
  7.9 46.5 %copy-start.2 = (f32[8,256]{1,0:T(8,128)S(1)}, f32[8,256]{1,0:T(8,128)}, u32[]{:S(2)}) copy-start(f32[8,256]{1,0:T(8,128)} %param.17) | copy-start | bytes 24580
  7.9 46.5 %copy-start.3 = (f32[8,256]{1,0:T(8,128)S(1)}, f32[8,256]{1,0:T(8,128)}, u32[]{:S(2)}) copy-start(f32[8,256]{1,0:T(8,128)} %param.14) | copy-start | bytes 24580

commit v4 on v3

--- a/solution.py
+++ b/solution.py
@@ -48,7 +48,7 @@
     own_cols = cols[pl.ds(pl.multiple_of(core * tokens, tokens), tokens), :]
     other_cols_ref[...] = cols[pl.ds(pl.multiple_of((1 - core) * tokens, tokens), tokens), :]
     copies[1].wait()
-    step = 256
+    step = 1024
     for at in range(0, own.shape[1], step):
         part_ref[at : at + step, :] = dot_over_tokens(own[:, at : at + step], own_cols)
     copies[2].wait()

time: 85.6 us -> 85.6 us (level)
  no operation moved by 1% of the time
where the time goes in v4:
time: 85.6 us; the launch traced here: 85.3 us
  blocking collectives  75.8 us (89%)
  Pallas kernels  5.55 us (6%)
  starting transfers between devices  1.92 us (2%)
  between operations  1.4 us (2%)
    all_to_all x1, blocking collectives, on_device(): far = lax.all_to_all(partial, FAR, 0, 0, tiled=True)  24.4 us
    all_to_all x1, blocking collectives, on_device(): near = lax.all_to_all(pieces, NEAR, 0, 0, tiled=True)  21.8 us
    all_to_all x1, blocking collectives, on_device(): lax.all_to_all(copies, FAR, 0, 0, tiled=True)  15.6 us
    all_to_all x1, blocking collectives, on_device(): weights = lax.all_to_all(copies, NEAR, 0, 0, tiled=True)  14 us
    pallas_call x1, Pallas kernels, on_device(): pl.pallas_call(functools.partial(gradient_kernel, sizes), out_shape=(jax....  2.67 us
    ppermute x1, starting transfers between devices, on_device(): other = lax.ppermute(normed, 'mp', [(0, 1), (1, 0)])  1.92 us
    pallas_call x1, Pallas kernels, on_device(): pl.pallas_call(own_half_kernel, out_shape=(jax.ShapeDtypeStruct((d, half_...  1.8 us
  transfers between devices with their start and end apart: 1, of which 0 were waited for; matrix products, arithmetic and copies ran while one was open for 0% of the time, Pallas kernels for 2%

profile of v4, /device:TPU:8, one launch (start us, length us, event | category | flops | bytes accessed | tf_op | source)
XLA Modules:
  0.0 85.3 jit_solution(17266454972615903481)
XLA Ops:
  0.6 1.9 %collective-permute-start = (bf16[192,2048]{1,0:T(8,128)(2,1)}, bf16[192,2048]{1,0:T(8,128)(2,1)S(1)}, u32[]{:S(2)}, u32[]{:S(2)}) collective-permute-start(bf16[192,2048]{1,0:T(8,128)(2,1)} %normed_ref.1), channel_id=1, source_target_pairs={{0,1},{1,0},{2,3},{3,2},{4,5},{5,4},{6,7},{7,6},{8,9},{9,8},{10,11... | collective-permute-start | bytes 2359304 | tf_op jit(solution)/shard_map/ppermute | solution.py:126
  3.2 1.8 %shard_map.136 = (f32[2048,256]{1,0:T(8,128)S(1)}, bf16[192,256]{1,0:T(8,128)(2,1)S(1)}, bf16[2048,256]{1,0:T(8,128)(2,1)S(1)}, f32[1,256]{1,0:T(1,128)S(1)}) custom-call(s32[1]{0:T(128)S(6)} %copy.17.flag_ref, s32[1,4]{1,0:T(1,128)} %mask_ref.1, bf16[192,2048]{1,0:T(8,128)(2,1)} %normed_ref.1, bf16[384,256]{1,0:T(8,128)(2,1)} %cols_ref.1, ...), custom_call_target="tpu_custom_call" | custom-call | tf_op jit(solution)/shard_map/pallas_call | solution.py:134
  5.0 0.0 collective-permute-done.other_ref
  5.0 2.7 %shard_map.137 = (f32[256,8,256]{2,1,0:T(8,128)S(1)}, bf16[2048,256]{1,0:T(8,128)(2,1)S(1)}, bf16[2048,256]{1,0:T(8,128)(2,1)}) custom-call(f32[2048,256]{1,0:T(8,128)S(1)} %get-tuple-element.19.part_ref, bf16[192,2048]{1,0:T(8,128)(2,1)S(1)} %collective-permute-done.other_ref, bf16[192,256]{1,0:T(8,128)(2,1)S(1)} %get-tuple-element.20.cols_ref, ...), custom_call_target="tpu_custom_call" | custom-call | tf_op jit(solution)/shard_map/pallas_call | solution.py:158
  7.7 0.2 convert_element_type.19
  7.9 0.0 copy-start
  7.9 0.0 copy-start.1
  7.9 0.0 copy-start.2
  7.9 0.0 copy-start.3
  8.0 21.8 %all_to_all.20 = f16[8,256,256]{2,1,0:T(8,128)(2,1)S(1)} all-to-all(f16[8,256,256]{2,1,0:T(8,128)(2,1)S(1)} %bitcast.9), channel_id=1, replica_groups=mesh['z'=8,'x'=4,'yh'=4,'yl'=2,'mp'=2] {'x','yl'}, dimensions={0} | all-to-all | bytes 2097152 | tf_op jit(solution)/shard_map/all_to_all | solution.py:171
  29.8 0.1 convert_reduce_fusion
  30.0 24.4 %all_to_all.21 = f16[32,8,256]{2,1,0:T(8,128)(2,1)S(1)} all-to-all(f16[32,8,256]{2,1,0:T(8,128)(2,1)S(1)} %fusion), channel_id=1, replica_groups=mesh['z'=8,'x'=4,'yh'=4,'yl'=2,'mp'=2] {'z','yh'}, dimensions={0} | all-to-all | bytes 262144 | tf_op jit(solution)/shard_map/all_to_all | solution.py:174
  54.5 0.0 copy-done
  54.5 0.0 copy-done.1
  54.5 0.0 copy-done.2
  54.5 0.0 copy-done.3
  54.6 15.6 %all_to_all.22 = bf16[32,8,256]{2,1,0:T(8,128)(2,1)S(1)} all-to-all(bf16[32,8,256]{2,1,0:T(8,128)(2,1)S(1)} %broadcast_in_dim.9), channel_id=1, replica_groups=mesh['z'=8,'x'=4,'yh'=4,'yl'=2,'mp'=2] {'z','yh'}, dimensions={0} | all-to-all | bytes 262144 | tf_op jit(solution)/shard_map/all_to_all | solution.py:185
  70.1 0.1 broadcast_in_dim.10
  70.2 14.0 %all_to_all.23 = bf16[8,256,256]{2,1,0:T(8,128)(2,1)S(1)} all-to-all(bf16[8,256,256]{2,1,0:T(8,128)(2,1)S(1)} %broadcast_in_dim.10), channel_id=1, replica_groups=mesh['z'=8,'x'=4,'yh'=4,'yl'=2,'mp'=2] {'x','yl'}, dimensions={0} | all-to-all | bytes 2097152 | tf_op jit(solution)/shard_map/all_to_all | solution.py:187
  84.2 1.1 %shard_map.138 = (bf16[8,4,4,2,8,256]{5,4,3,2,1,0:T(8,128)(2,1)}, bf16[2048,256]{1,0:T(8,128)(2,1)}, f32[8,256]{1,0:T(8,128)}, f32[8,256]{1,0:T(8,128)}, f32[8,256]{1,0:T(8,128)}, /*index=5*/f32[8,256]{1,0:T(8,128)}) custom-call(bf16[8,8,4,8,256]{4,3,2,1,0:T(8,128)(2,1)S(1)} %bitcast.8, ...), custom_call_target="tpu_custom_call", output_to_operand_aliasing={{1}: (2, {})} | custom-call | tf_op jit(solution)/shard_map/pallas_call | solution.py:190
  (4 shorter events, 0.1 us)
Async XLA Ops:
  0.6 4.4 %collective-permute-start = (bf16[192,2048]{1,0:T(8,128)(2,1)}, bf16[192,2048]{1,0:T(8,128)(2,1)S(1)}, u32[]{:S(2)}, u32[]{:S(2)}) collective-permute-start(bf16[192,2048]{1,0:T(8,128)(2,1)} %normed_ref.1), channel_id=1, source_target_pairs={{0,1},{1,0},{2,3},{3,2},{4,5},{5,4},{6,7},{7,6},{8,9},{9,8},{10,11... | collective-permute-start | bytes 2359304 | tf_op jit(solution)/shard_map/ppermute | solution.py:126
  7.9 46.6 %copy-start = (f32[8,256]{1,0:T(8,128)S(1)}, f32[8,256]{1,0:T(8,128)}, u32[]{:S(2)}) copy-start(f32[8,256]{1,0:T(8,128)} %param.15) | copy-start | bytes 24580
  7.9 46.5 %copy-start.1 = (f32[8,256]{1,0:T(8,128)S(1)}, f32[8,256]{1,0:T(8,128)}, u32[]{:S(2)}) copy-start(f32[8,256]{1,0:T(8,128)} %param.16) | copy-start | bytes 24580
  7.9 46.5 %copy-start.2 = (f32[8,256]{1,0:T(8,128)S(1)}, f32[8,256]{1,0:T(8,128)}, u32[]{:S(2)}) copy-start(f32[8,256]{1,0:T(8,128)} %param.17) | copy-start | bytes 24580
  7.9 46.5 %copy-start.3 = (f32[8,256]{1,0:T(8,128)S(1)}, f32[8,256]{1,0:T(8,128)}, u32[]{:S(2)}) copy-start(f32[8,256]{1,0:T(8,128)} %param.14) | copy-start | bytes 24580
